TPU v7x, 32 devices: a 4x4x1 block of a 4x4x8 slice. The times are simulated.
32 devices in a mesh: dp: 1 (over z), pz: 4 (over y), py: 8 (over x, core).
Axes of the slice: x: 4, y: 4, z: 1, core: 2. Of those that a mesh axis runs over, the one named last changes fastest.
The devices are a block of a 4x4x8 slice.
Arguments:
- rho_re: float32 [24, 128, 128, 128], P('dp', None, 'py', 'pz')
- rho_im: float32 [24, 128, 128, 128], P('dp', None, 'py', 'pz')
- g_re: float32 [128, 128, 128], P('py', 'pz')
- g_im: float32 [128, 128, 128], P('py', 'pz')
Outputs:
- output 1: float32 [24, 128, 128, 128], P('dp', None, 'py', 'pz')
- output 2: float32 [24, 128, 128, 128], P('dp', None, 'py', 'pz')
- output 3: float32 [24, 128, 128, 128], P('dp', 'py', 'pz')
- output 4: float32 [24, 128, 128, 128], P('dp', 'py', 'pz')
All inputs are finite; a program needn't handle non-finite values.
Results may differ from a plain program's by a relative error of at most 0.001.
Values sent between devices are 32-bit elements.
A program may use at most 768 MiB of HBM per device.

v0:
```python
import jax
import jax.numpy as jnp
from jax import lax
from jax.sharding import PartitionSpec as P


def regroup(volume, axis_name, split_dim, concat_dim):
    halves = jnp.stack([jnp.real(volume), jnp.imag(volume)])
    arrived = lax.all_to_all(halves, axis_name, split_dim + 1, concat_dim + 1, tiled=True)
    return lax.complex(arrived[0], arrived[1])


def solution(mesh):
    def local_solve(rho_re, rho_im, g_re, g_im):
        volume = jnp.fft.fft(lax.complex(rho_re, rho_im), axis=1, norm="ortho")
        volume = regroup(volume, "py", 1, 2)
        volume = jnp.fft.fft(volume, axis=2, norm="ortho")
        volume = regroup(volume, "pz", 2, 3)
        spectrum = jnp.fft.fft(volume, axis=3, norm="ortho") * lax.complex(g_re, g_im)
        volume = jnp.fft.ifft(spectrum, axis=3, norm="ortho")
        volume = regroup(volume, "pz", 3, 2)
        volume = jnp.fft.ifft(volume, axis=2, norm="ortho")
        volume = regroup(volume, "py", 2, 1)
        volume = jnp.fft.ifft(volume, axis=1, norm="ortho")
        return jnp.real(volume), jnp.imag(volume), jnp.real(spectrum), jnp.imag(spectrum)

    space_layout = P("dp", None, "py", "pz")
    wave_layout = P("dp", "py", "pz", None)
    green_layout = P("py", "pz", None)
    return jax.shard_map(local_solve, mesh=mesh,
                         in_specs=(space_layout, space_layout, green_layout, green_layout),
                         out_specs=(space_layout, space_layout, wave_layout, wave_layout),
                         check_vma=False)
```

profile of v0, /device:TPU:97, one launch (start us, length us, event | category | flops | bytes accessed | tf_op | source)
XLA Modules:
  0.0 2038.6 jit_solution(1820719055714492652)
XLA Ops:
  38.6 50.1 %copy.42 = f32[2,24,128,16,32]{4,3,1,0,2:T(8,128)} copy(f32[2,24,128,16,32]{2,4,3,1,0:T(8,128)} %pad_maximum_fusion) | data formatting | bytes 25165824 | tf_op jit(solution)/shard_map/stack | solution.py:8
  88.7 53.5 %reshape.98 = f32[8,1,393216]{2,1,0:T(1,128)} reshape(f32[128,2,24,16,32]{4,3,2,1,0:T(8,128)} %bitcast.311) | data formatting | bytes 25165824
  142.2 147.1 %all_to_all.56 = f32[8,1,393216]{2,1,0:T(1,128)} all-to-all(f32[8,1,393216]{2,1,0:T(1,128)} %reshape.98), channel_id=1, replica_groups=mesh['dp'=1,'pz'=4,'py'=8] {'py'}, dimensions={0} | all-to-all | bytes 25165824 | tf_op jit(solution)/shard_map/all_to_all | solution.py:9
  289.8 36.5 %reduce.6 = f32[8,393216]{1,0:T(8,128)} reduce(f32[8,1,393216]{2,1,0:T(1,128)} %all_to_all.56, f32[]{:T(128)} %broadcast.228), dimensions={1}, to_apply=%all_to_all.40.reduce_sub_computation | reduce | bytes 25165828 | tf_op jit(solution)/shard_map/all_to_all | solution.py:9
  326.3 42.3 %reshape.99 = f32[128,2,24,16,32]{4,3,2,1,0:T(8,128)} reshape(f32[8,393216]{1,0:T(8,128)} %reduce.6) | data formatting | bytes 25165824
  368.6 34.2 %copy.43 = f32[2,24,128,16,32]{4,3,2,1,0:T(8,128)} copy(f32[2,24,128,16,32]{4,3,1,0,2:T(8,128)} %bitcast.307) | data formatting | bytes 25165824 | tf_op jit(solution)/shard_map/all_to_all | solution.py:9
  402.8 31.9 %fusion.157 = (f32[1,24,16,8,16,32]{5,4,2,3,1,0:T(8,128)}, f32[1,24,16,8,16,32]{5,4,2,3,1,0:T(8,128)}) fusion(f32[2,24,16,8,16,32]{5,4,2,3,1,0:T(8,128)} %bitcast.303), kind=kLoop, calls=%fused_computation.180 | loop fusion | bytes 25165824 | tf_op jit(solution)/shard_map/slice | solution.py:10
  540.2 38.4 %copy.48 = f32[2,24,16,128,32]{4,2,1,0,3:T(8,128)} copy(f32[2,24,16,128,32]{3,4,2,1,0:T(8,128)} %pad_maximum_fusion.1) | data formatting | bytes 25165824 | tf_op jit(solution)/shard_map/stack | solution.py:8
  578.6 47.0 %reshape.100 = f32[4,1,786432]{2,1,0:T(1,128)} reshape(f32[128,2,24,16,32]{4,3,2,1,0:T(8,128)} %bitcast.312) | data formatting | bytes 25165824
  632.0 138.4 %all-to-all-done.1 = f32[4,1,786432]{2,1,0:T(1,128)} async-done(((f32[4,1,786432]{2,1,0:T(1,128)}), f32[4,1,786432]{2,1,0:T(1,128)}, u32[]{:S(2)}, u32[]{:S(2)}) %all-to-all-start.1) | async-done | bytes 12582944 | tf_op jit(solution)/shard_map/all_to_all | solution.py:9
  770.4 39.9 %reduce.7 = f32[4,786432]{1,0:T(4,128)} reduce(f32[4,1,786432]{2,1,0:T(1,128)} %all-to-all-done.1, f32[]{:T(128)} %broadcast.228), dimensions={1}, to_apply=%all_to_all.43.reduce_sub_computation | reduce | bytes 25165828 | tf_op jit(solution)/shard_map/all_to_all | solution.py:9
  810.3 49.8 %reshape.101 = f32[128,2,24,16,32]{4,3,2,1,0:T(8,128)} reshape(f32[4,786432]{1,0:T(4,128)} %reduce.7) | data formatting | bytes 25165824
  860.1 55.5 %copy.73 = f32[2,24,16,4,32,32]{5,3,4,2,1,0:T(4,128)} copy(f32[2,24,16,4,32,32]{5,2,1,0,4,3:T(8,128)} %bitcast.308) | data formatting | bytes 25165824 | tf_op jit(solution)/shard_map/all_to_all | solution.py:9
  915.6 33.5 %fusion.156 = (f32[1,24,16,32,4,32]{5,4,3,2,1,0:T(4,128)}, f32[1,24,16,32,4,32]{5,4,3,2,1,0:T(4,128)}) fusion(f32[2,24,16,32,4,32]{5,4,3,2,1,0:T(4,128)} %bitcast.304), kind=kLoop, calls=%fused_computation.179 | loop fusion | bytes 25165824 | tf_op jit(solution)/shard_map/slice | solution.py:10
  949.1 19.6 squeeze.27
  968.7 19.6 squeeze.26
  1058.4 38.4 %copy.50 = f32[2,24,16,32,128]{3,2,1,0,4:T(8,128)} copy(f32[2,24,16,32,128]{4,3,2,1,0:T(8,128)} %pad_maximum_fusion.2) | data formatting | bytes 25165824 | tf_op jit(solution)/shard_map/stack | solution.py:8
  1096.8 47.0 %reshape.102 = f32[4,1,786432]{2,1,0:T(1,128)} reshape(f32[128,2,24,16,32]{4,3,2,1,0:T(8,128)} %bitcast.313) | data formatting | bytes 25165824
  1143.8 146.0 %all_to_all.57 = f32[4,1,786432]{2,1,0:T(1,128)} all-to-all(f32[4,1,786432]{2,1,0:T(1,128)} %reshape.102), channel_id=1, replica_groups=mesh['dp'=1,'pz'=4,'py'=8] {'pz'}, dimensions={0} | all-to-all | bytes 25165824 | tf_op jit(solution)/shard_map/all_to_all | solution.py:9
  1289.7 39.9 %reduce.8 = f32[4,786432]{1,0:T(4,128)} reduce(f32[4,1,786432]{2,1,0:T(1,128)} %all_to_all.57, f32[]{:T(128)} %broadcast.228), dimensions={1}, to_apply=%all_to_all.46.reduce_sub_computation | reduce | bytes 25165828 | tf_op jit(solution)/shard_map/all_to_all | solution.py:9
  1329.6 49.8 %reshape.103 = f32[128,2,24,16,32]{4,3,2,1,0:T(8,128)} reshape(f32[4,786432]{1,0:T(4,128)} %reduce.8) | data formatting | bytes 25165824
  1379.4 55.5 %copy.72 = f32[2,24,16,32,4,32]{3,4,5,2,1,0:T(4,128)} copy(f32[2,24,16,32,4,32]{3,2,1,0,5,4:T(8,128)} %bitcast.309) | data formatting | bytes 25165824 | tf_op jit(solution)/shard_map/all_to_all | solution.py:9
  1434.9 33.5 %fusion.155 = (f32[1,24,16,4,32,32]{4,3,5,2,1,0:T(4,128)}, f32[1,24,16,4,32,32]{4,3,5,2,1,0:T(4,128)}) fusion(f32[2,24,16,4,32,32]{4,3,5,2,1,0:T(4,128)} %bitcast.305), kind=kLoop, calls=%fused_computation.178 | loop fusion | bytes 25165824 | tf_op jit(solution)/shard_map/slice | solution.py:10
  1468.5 19.6 squeeze.28
  1488.1 19.6 squeeze.29
  1546.3 38.4 %copy.52 = f32[2,24,16,128,32]{4,2,1,0,3:T(8,128)} copy(f32[2,24,16,128,32]{3,4,2,1,0:T(8,128)} %pad_maximum_fusion.3) | data formatting | bytes 25165824 | tf_op jit(solution)/shard_map/stack | solution.py:8
  1584.7 53.6 %reshape.104 = f32[8,1,393216]{2,1,0:T(1,128)} reshape(f32[128,2,24,16,32]{4,3,2,1,0:T(8,128)} %bitcast.314) | data formatting | bytes 25165824
  1638.3 147.8 %all_to_all.58 = f32[8,1,393216]{2,1,0:T(1,128)} all-to-all(f32[8,1,393216]{2,1,0:T(1,128)} %reshape.104), channel_id=1, replica_groups=mesh['dp'=1,'pz'=4,'py'=8] {'py'}, dimensions={0} | all-to-all | bytes 25165824 | tf_op jit(solution)/shard_map/all_to_all | solution.py:9
  1786.1 36.5 %reduce.9 = f32[8,393216]{1,0:T(8,128)} reduce(f32[8,1,393216]{2,1,0:T(1,128)} %all_to_all.58, f32[]{:T(128)} %broadcast.228), dimensions={1}, to_apply=%all_to_all.49.reduce_sub_computation | reduce | bytes 25165828 | tf_op jit(solution)/shard_map/all_to_all | solution.py:9
  1822.6 42.3 %reshape.105 = f32[128,2,24,16,32]{4,3,2,1,0:T(8,128)} reshape(f32[8,393216]{1,0:T(8,128)} %reduce.9) | data formatting | bytes 25165824
  1864.9 45.9 %copy.53 = f32[2,24,16,128,32]{4,3,2,1,0:T(8,128)} copy(f32[2,24,16,128,32]{4,2,1,0,3:T(8,128)} %bitcast.310) | data formatting | bytes 25165824 | tf_op jit(solution)/shard_map/all_to_all | solution.py:9
  1910.8 31.5 %fusion.154 = (f32[1,24,8,16,16,32]{5,4,2,3,1,0:T(8,128)}, f32[1,24,8,16,16,32]{5,4,2,3,1,0:T(8,128)}) fusion(f32[2,24,8,16,16,32]{5,4,2,3,1,0:T(8,128)} %bitcast.306), kind=kLoop, calls=%fused_computation.177 | loop fusion | bytes 25165824 | tf_op jit(solution)/shard_map/slice | solution.py:10
  (58 shorter events, 354.9 us)
Async XLA Ops:
  0.6 10.2 copy-start.9
  0.6 10.2 copy-start.10
  503.0 10.3 copy-start.3
  503.0 10.3 copy-start.8
  625.6 144.8 %all-to-all-start.1 = ((f32[4,1,786432]{2,1,0:T(1,128)}), f32[4,1,786432]{2,1,0:T(1,128)}, u32[]{:S(2)}, u32[]{:S(2)}) async-start(f32[4,1,786432]{2,1,0:T(1,128)} %reshape.100), calls=%async_computation.1 | async-start | bytes 25165824 | tf_op jit(solution)/shard_map/all_to_all | solution.py:9
  988.3 9.5 copy-start.2
  997.9 7.4 copy-start.11
  997.9 7.4 copy-start.12
  1020.7 6.1 copy-start
  1020.8 13.6 copy-start.1
  1507.7 10.6 copy-start.4
  1507.7 10.6 copy-start.7
  2011.8 10.3 copy-start.5
  2011.8 10.3 copy-start.6
where the time goes:
time: 2050 us; the launch traced here: 2040 us
  local copies, waits for them, and re-layouts  1090 us (53%)
  blocking collectives  441 us (22%)
  other arithmetic  197 us (10%)
  matrix products  166 us (8%)
  waiting for transfers between devices  138 us (7%)
    all_to_all x3, blocking collectives, regroup(): lax.all_to_all(halves, axis_name, split_dim + 1, concat_dim + 1, tiled=True)  441 us
    unnamed x34, local copies, waits for them, and re-layouts  385 us
    slice x8, local copies, waits for them, and re-layouts, regroup(): return lax.complex(arrived[0], arrived[1])  201 us
    all_to_all x5, local copies, waits for them, and re-layouts, regroup(): lax.all_to_all(halves, axis_name, split_dim + 1, concat_dim + 1, tiled=True)  192 us
    another operation x4, local copies, waits for them, and re-layouts, regroup(): halves = jnp.stack([jnp.real(volume), jnp.imag(volume)])  165 us
    all_to_all x4, other arithmetic, regroup(): lax.all_to_all(halves, axis_name, split_dim + 1, concat_dim + 1, tiled=True)  153 us
    squeeze x8, local copies, waits for them, and re-layouts, regroup(): return lax.complex(arrived[0], arrived[1])  146 us
    all_to_all x1, waiting for transfers between devices, regroup(): lax.all_to_all(halves, axis_name, split_dim + 1, concat_dim + 1, tiled=True)  138 us
  transfers between devices with their start and end apart: 1, of which 1 were waited for; matrix products, arithmetic and copies ran while one was open for 0% of the time, Pallas kernels for 0%

commit v1 on v0

v1 whole, which is shorter than its diff:
```python
import functools

import jax
import jax.numpy as jnp
import numpy as np
from jax import lax
from jax.experimental import pallas as pl
from jax.experimental.pallas import tpu as pltpu
from jax.sharding import PartitionSpec as P

MESH = pl.DeviceIdType.MESH
HIGHEST = lax.Precision.HIGHEST


def dft(n, sign):
    angle = 2.0 * np.pi * (np.outer(np.arange(n), np.arange(n)) % n) / n
    cos, sin = np.cos(angle) / np.sqrt(n), sign * np.sin(angle) / np.sqrt(n)
    return np.block([[cos, -sin], [sin, cos]])


def order(n, dims, perm):
    return np.arange(2 * n).reshape((2,) + dims).transpose(perm).reshape(-1)


def swap_blocks(a, lane):
    a = list(a)
    for d, pairs in ((64, ((0, 2), (1, 3))), (32, ((0, 1), (2, 3)))):
        low = (lane // d) % 2 == 0
        for i, j in pairs:
            u, v = a[i], a[j]
            a[i] = jnp.where(low, u, pltpu.roll(v, d, 1))
            a[j] = jnp.where(low, pltpu.roll(u, 128 - d, 1), v)
    return a


def kernel(fields, npy, npz, rho_re, rho_im, g_re, g_im, w1, w2, w3, w4, w5, w6,
           phi_re, phi_im, hat_re, hat_im,
           rho, hat, phi, work, send1, send2, send3, send4, recv1, recv2, recv3, recv4,
           in_sem, hat_sem, phi_sem, send_sem, recv_sem):
    py, pz = lax.axis_index("py"), lax.axis_index("pz")
    xrows, yrows = recv1.shape[1] // npy, recv2.shape[1] // npz
    lane = lax.broadcasted_iota(jnp.int32, (32, 128), 1)

    barrier = pltpu.get_barrier_semaphore()
    for j in range(1, npy):
        pl.semaphore_signal(barrier, inc=1, device_id={"py": lax.rem(py + j, npy)}, device_id_type=MESH)
    for j in range(1, npz):
        pl.semaphore_signal(barrier, inc=1, device_id={"pz": lax.rem(pz + j, npz)}, device_id_type=MESH)
    pl.semaphore_wait(barrier, npy + npz - 2)

    def load(f, slot):
        return [pltpu.make_async_copy(src.at[f], rho.at[slot, c], in_sem.at[slot, c])
                for c, src in enumerate((rho_re, rho_im))]

    def store(dsts, buf, sem, f, slot):
        return [pltpu.make_async_copy(buf.at[slot, c], dst.at[f], sem.at[slot, c]) for c, dst in enumerate(dsts)]

    def exchange(stage, axis, send, recv, f, slot):
        me, n, rows = (py, npy, xrows) if axis == "py" else (pz, npz, yrows)
        mine = pl.ds(pl.multiple_of(me * rows, rows), rows)
        for j in range(1, n):
            to = lax.rem(me + j, n)
            pltpu.make_async_remote_copy(
                src_ref=send.at[slot, pl.ds(pl.multiple_of(to * rows, rows), rows), :], dst_ref=recv.at[f, mine, :],
                send_sem=send_sem.at[stage, slot], recv_sem=recv_sem.at[stage, f],
                device_id={axis: to}, device_id_type=MESH).start()
        pltpu.make_async_copy(send.at[slot, mine, :], recv.at[f, mine, :], recv_sem.at[stage, f]).start()

    def wait_sent(stage, send, slot, rows):
        part = send.at[slot, pl.ds(0, send.shape[1] - rows), :]
        pltpu.make_async_copy(part, part, send_sem.at[stage, slot]).wait()

    def wait_received(stage, recv, f):
        pltpu.make_async_copy(recv.at[f], recv.at[f], recv_sem.at[stage, f]).wait()

    for cp in load(0, 0):
        cp.start()

    def step(s, carry):
        @pl.when(s < fields)
        def _():
            f, slot = s, lax.rem(s, 2)

            @pl.when(f + 1 < fields)
            def _():
                for cp in load(f + 1, 1 - slot):
                    cp.start()
            for cp in load(f, slot):
                cp.wait()

            @pl.when(f >= 2)
            def _():
                wait_sent(0, send1, slot, xrows)
            volume = jnp.concatenate([rho[slot, 0], rho[slot, 1]], axis=1)
            out = lax.dot_general(w1[...], volume, (((1,), (1,)), ((), ())), precision=HIGHEST,
                                  preferred_element_type=jnp.float32)
            for p in range(8):
                for t in range(4):
                    send1[slot, p * 128 + t * 32:p * 128 + (t + 1) * 32, :] = out[p * 32:(p + 1) * 32, t * 128:(t + 1) * 128]
            exchange(0, "py", send1, recv1, f, slot)

        @pl.when((s >= 1) & (s < fields + 1))
        def _():
            f = s - 1
            slot = lax.rem(f, 2)
            wait_received(0, recv1, f)
            for c in range(2):
                for g in range(4):
                    blocks = [recv1[f, pl.ds(c * 16 + 4 * g + k, 32, stride=32), :] for k in range(4)]
                    for y, b in enumerate(swap_blocks(blocks, lane)):
                        work[c * 128 + y * 32:c * 128 + (y + 1) * 32, g * 128:(g + 1) * 128] = b

            @pl.when(f >= 2)
            def _():
                wait_sent(1, send2, slot, yrows)
            send2[slot] = jnp.dot(w2[...], work[...], precision=HIGHEST, preferred_element_type=jnp.float32)
            exchange(1, "pz", send2, recv2, f, slot)

        @pl.when((s >= 2) & (s < fields + 2))
        def _():
            f = s - 2
            slot = lax.rem(f, 2)
            wait_received(1, recv2, f)
            cols = []
            for c in range(2):
                rows = []
                for g in range(4):
                    blocks = [recv2[f, b * 64 + c * 32:b * 64 + (c + 1) * 32, g * 128:(g + 1) * 128] for b in range(4)]
                    rows += swap_blocks(blocks, lane)
                cols.append(jnp.concatenate(rows, axis=0))
            spec = jnp.dot(jnp.concatenate(cols, axis=1), w3[...], precision=HIGHEST, preferred_element_type=jnp.float32)
            sr, si = spec[:, :128], spec[:, 128:]

            @pl.when(f >= 2)
            def _():
                for cp in store((hat_re, hat_im), hat, hat_sem, f, slot):
                    cp.wait()
                wait_sent(2, send3, slot, yrows)
            hat[slot, 0] = sr * g_re[...] - si * g_im[...]
            hat[slot, 1] = sr * g_im[...] + si * g_re[...]
            for cp in store((hat_re, hat_im), hat, hat_sem, f, slot):
                cp.start()
            back = jnp.dot(jnp.concatenate([hat[slot, 0], hat[slot, 1]], axis=1), w4[...], precision=HIGHEST,
                           preferred_element_type=jnp.float32)
            for c in range(2):
                for g in range(4):
                    blocks = [back[(4 * g + k) * 32:(4 * g + k + 1) * 32, c * 128:(c + 1) * 128] for k in range(4)]
                    for b, block in enumerate(swap_blocks(blocks, lane)):
                        send3[slot, b * 64 + c * 32:b * 64 + (c + 1) * 32, g * 128:(g + 1) * 128] = block
            exchange(2, "pz", send3, recv3, f, slot)

        @pl.when((s >= 3) & (s < fields + 3))
        def _():
            f = s - 3
            slot = lax.rem(f, 2)
            wait_received(2, recv3, f)

            @pl.when(f >= 2)
            def _():
                wait_sent(3, send4, slot, xrows)
            back = jnp.dot(w5[...], recv3[f], precision=HIGHEST, preferred_element_type=jnp.float32)
            for c in range(2):
                for g in range(4):
                    blocks = [back[c * 128 + y * 32:c * 128 + (y + 1) * 32, g * 128:(g + 1) * 128] for y in range(4)]
                    for k, block in enumerate(swap_blocks(blocks, lane)):
                        send4[slot, pl.ds(c * 16 + 4 * g + k, 32, stride=32), :] = block
            exchange(3, "py", send4, recv4, f, slot)

        @pl.when(s >= 4)
        def _():
            f = s - 4
            slot = lax.rem(f, 2)
            wait_received(3, recv4, f)

            @pl.when(f >= 2)
            def _():
                for cp in store((phi_re, phi_im), phi, phi_sem, f, slot):
                    cp.wait()
            lines = []
            for t in range(4):
                block = jnp.concatenate([recv4[f, p * 128 + t * 32:p * 128 + (t + 1) * 32, :] for p in range(8)], axis=0)
                lines.append(block.T)
            out = jnp.dot(jnp.concatenate(lines, axis=0), w6[...], precision=HIGHEST, preferred_element_type=jnp.float32)
            phi[slot, 0] = out[:, :128]
            phi[slot, 1] = out[:, 128:]
            for cp in store((phi_re, phi_im), phi, phi_sem, f, slot):
                cp.start()

        return carry

    lax.fori_loop(0, fields + 4, step, 0)
    for slot in range(2):
        for cp in store((hat_re, hat_im), hat, hat_sem, 0, slot) + store((phi_re, phi_im), phi, phi_sem, 0, slot):
            cp.wait()
        wait_sent(0, send1, slot, xrows)
        wait_sent(1, send2, slot, yrows)
        wait_sent(2, send3, slot, yrows)
        wait_sent(3, send4, slot, xrows)


def solution(mesh):
    npy, npz = mesh.shape["py"], mesh.shape["pz"]

    def local_solve(rho_re, rho_im, g_re, g_im):
        fields, n, ny, nz = rho_re.shape
        kx, ky = n // npy, n // npz
        fwd, inv = dft(n, -1), dft(n, 1)
        natural = np.arange(2 * n)
        x_blocks = order(n, (npy, kx), (1, 0, 2))
        y_blocks = order(n, (npz, ky), (1, 0, 2))
        y_mixed = order(n, (npy, ny // 4, 4), (0, 3, 1, 2))
        pick = lambda m, r, c: jnp.asarray(m[np.ix_(r, c)].astype(np.float32))
        mats = (pick(fwd, x_blocks, natural), pick(fwd, y_blocks, y_mixed), pick(fwd, natural, natural).T,
                pick(inv, natural, natural).T, pick(inv, y_mixed, y_blocks), pick(inv, natural, x_blocks).T)
        lines = ny * nz
        space = lambda v: v.transpose(0, 2, 3, 1).reshape(fields, lines, n)
        sent = 2 * lines
        f32 = jnp.float32
        out = pl.pallas_call(
            functools.partial(kernel, fields, npy, npz),
            out_shape=[jax.ShapeDtypeStruct((fields, lines, n), f32)] * 4,
            in_specs=[pl.BlockSpec(memory_space=pl.ANY)] * 2 + [pl.BlockSpec(memory_space=pltpu.VMEM)] * 8,
            out_specs=[pl.BlockSpec(memory_space=pl.ANY)] * 4,
            scratch_shapes=[
                pltpu.VMEM((2, 2, lines, n), f32), pltpu.VMEM((2, 2, lines, n), f32), pltpu.VMEM((2, 2, lines, n), f32),
                pltpu.VMEM((2 * n, lines), f32),
                pltpu.VMEM((2, sent, n), f32), pltpu.VMEM((2, 2 * n, lines), f32),
                pltpu.VMEM((2, 2 * n, lines), f32), pltpu.VMEM((2, sent, n), f32),
                pltpu.VMEM((fields, sent, n), f32), pltpu.VMEM((fields, 2 * n, lines), f32),
                pltpu.VMEM((fields, 2 * n, lines), f32), pltpu.VMEM((fields, sent, n), f32),
                pltpu.SemaphoreType.DMA((2, 2)), pltpu.SemaphoreType.DMA((2, 2)), pltpu.SemaphoreType.DMA((2, 2)),
                pltpu.SemaphoreType.DMA((4, 2)), pltpu.SemaphoreType.DMA((4, fields)),
            ],
            compiler_params=pltpu.CompilerParams(collective_id=0, has_side_effects=True, vmem_limit_bytes=67043328),
        )(space(rho_re), space(rho_im), g_re.reshape(lines, n), g_im.reshape(lines, n), *mats)
        grid = lambda v: v.reshape(fields, ny, nz, n).transpose(0, 3, 1, 2)
        wave = lambda v: v.reshape(fields, kx, ky, n)
        return grid(out[0]), grid(out[1]), wave(out[2]), wave(out[3])

    space_layout = P("dp", None, "py", "pz")
    wave_layout = P("dp", "py", "pz", None)
    green_layout = P("py", "pz", None)
    return jax.shard_map(local_solve, mesh=mesh,
                         in_specs=(space_layout, space_layout, green_layout, green_layout),
                         out_specs=(space_layout, space_layout, wave_layout, wave_layout),
                         check_vma=False)
```

time: 2050 us -> 325 us (0.16)
  local copies, waits for them, and re-layouts: 1090 us -> 17.7 us
  blocking collectives: 441 us -> 0 us
  Pallas kernels: 0 us -> 307 us
  other arithmetic: 197 us -> 0.01 us
  matrix products: 166 us -> 0 us
  waiting for transfers between devices: 138 us -> 0 us
    all_to_all x3 -> x0, blocking collectives: 441 us -> none  [regroup(): lax.all_to_all(halves, axis_name, split_dim + 1, concat_dim + 1, tiled=True)]
    unnamed x34 -> x14, local copies, waits for them, and re-layouts: 385 us -> 17.7 us
    pallas_call x0 -> x1, Pallas kernels: none -> 307 us  [local_solve(): pl.pallas_call(functools.partial(kernel, fields, npy, npz), out_shape=[ja...]
    slice x8 -> x0, local copies, waits for them, and re-layouts: 201 us -> none  [regroup(): return lax.complex(arrived[0], arrived[1])]
    all_to_all x5 -> x0, local copies, waits for them, and re-layouts: 192 us -> none  [regroup(): lax.all_to_all(halves, axis_name, split_dim + 1, concat_dim + 1, tiled=True)]
    another operation x18 -> x0, matrix products: 166 us -> none  [the longest x3 32.4 us: local_solve(): jnp.fft.fft(volume, axis=3, norm='ortho') * lax.complex(g_re, g_im)]
    another operation x4 -> x0, local copies, waits for them, and re-layouts: 165 us -> none  [regroup(): halves = jnp.stack([jnp.real(volume), jnp.imag(volume)])]
    all_to_all x4 -> x0, other arithmetic: 153 us -> none  [regroup(): lax.all_to_all(halves, axis_name, split_dim + 1, concat_dim + 1, tiled=True)]
  transfers between devices with their start and end apart: 1 -> 0, of which waited for: 1 -> 0; matrix products, arithmetic and copies ran while one was open for 0% -> 0% of each run, Pallas kernels for 0% -> 0%
where the time goes in v1:
time: 325 us
  Pallas kernels  307 us (94%)
  local copies, waits for them, and re-layouts  17.7 us (5%)
    pallas_call x1, Pallas kernels, local_solve(): pl.pallas_call(functools.partial(kernel, fields, npy, npz), out_shape=[ja...  307 us
    unnamed x14, local copies, waits for them, and re-layouts  17.7 us

profile of v1, /device:TPU:97, one launch (start us, length us, event | category | flops | bytes accessed | tf_op | source)
XLA Modules:
  0.0 325.1 jit_solution(1953499311386973181)
XLA Ops:
  0.6 306.8 %shard_map.129 = (f32[24,512,128]{2,1,0:T(8,128)}, f32[24,512,128]{2,1,0:T(8,128)}, f32[24,512,128]{2,1,0:T(8,128)}, f32[24,512,128]{2,1,0:T(8,128)}) custom-call(f32[24,512,128]{2,1,0:T(8,128)} %bitcast.16, f32[24,512,128]{2,1,0:T(8,128)} %bitcast.17, f32[512,128]{1,0:T(8,128)} %bitcast.26, f32[512,128]{1,0:T(8,128)} %bitcast.27, ...), custom_call_target="tpu_custom_call" | custom-call | tf_op jit(solution)/shard_map/pallas_call | solution.py:219
  307.4 0.0 copy-start
  307.4 0.0 slice-start.2
  307.4 7.0 %copy.18 = f32[24,128,16,32]{1,3,2,0:T(8,128)} copy(f32[24,128,16,32]{1,3,2,0:T(8,128)} %bitcast.25) | data formatting | bytes 12582912
  314.5 0.0 copy-done
  314.5 0.0 slice-start.3
  314.5 0.0 slice-start
  314.5 3.2 copy.19
  317.7 0.0 slice-done.2
  317.7 0.0 slice-done.3
  317.7 0.0 slice-start.1
  317.7 3.2 copy.20
  320.9 0.9 slice-done
  321.8 0.7 slice-done.1
  322.4 2.7 copy.21
  (2 shorter events, 0.0 us)
Async XLA Ops:
  307.4 7.1 %copy-start = (f32[24,512,128]{2,1,0:T(8,128)S(1)}, f32[24,512,128]{2,1,0:T(8,128)}, u32[]{:S(2)}) copy-start(f32[24,512,128]{2,1,0:T(8,128)} %get-tuple-element.9) | copy-start | bytes 18874372
  307.4 10.3 %slice-start.2 = ((s8[6291456]{0:T(1024)(128)(4,1)}), s8[4194304]{0:T(1024)(128)(4,1)S(1)}, s32[]{:S(2)}) async-start(s8[6291456]{0:T(1024)(128)(4,1)} %bitcast.21), calls=%async_computation.2 | async-start | bytes 8388608
  314.5 3.2 slice-start.3
  314.5 7.3 %slice-start = ((s8[6291456]{0:T(1024)(128)(4,1)}), s8[4194304]{0:T(1024)(128)(4,1)S(1)}, s32[]{:S(2)}) async-start(s8[6291456]{0:T(1024)(128)(4,1)} %bitcast.18), calls=%async_computation | async-start | bytes 8388608
  317.7 4.7 %slice-start.1 = ((s8[6291456]{0:T(1024)(128)(4,1)}), s8[2097152]{0:T(1024)(128)(4,1)S(1)}, s32[]{:S(2)}) async-start(s8[6291456]{0:T(1024)(128)(4,1)} %bitcast.18), calls=%async_computation.1 | async-start | bytes 4194304

commit v2 on v1

v2 whole, which is shorter than its diff:
```python
import functools

import jax
import jax.numpy as jnp
import numpy as np
from jax import lax
from jax.experimental import pallas as pl
from jax.experimental.pallas import tpu as pltpu
from jax.sharding import PartitionSpec as P

MESH = pl.DeviceIdType.MESH
HIGHEST = lax.Precision.HIGHEST
RING = 8
SLOTS = 4


def dft(n, sign):
    angle = 2.0 * np.pi * (np.outer(np.arange(n), np.arange(n)) % n) / n
    cos, sin = np.cos(angle) / np.sqrt(n), sign * np.sin(angle) / np.sqrt(n)
    return np.block([[cos, -sin], [sin, cos]])


def order(n, dims, perm):
    return np.arange(2 * n).reshape((2,) + dims).transpose(perm).reshape(-1)


def swap_blocks(a, lane):
    a = list(a)
    for d, pairs in ((64, ((0, 2), (1, 3))), (32, ((0, 1), (2, 3)))):
        low = (lane // d) % 2 == 0
        for i, j in pairs:
            u, v = a[i], a[j]
            a[i] = jnp.where(low, u, pltpu.roll(v, d, 1))
            a[j] = jnp.where(low, pltpu.roll(u, 128 - d, 1), v)
    return a


def kernel(fields, npy, npz, rho_re, rho_im, green_re, green_im, m1, m2, m3, m4, m5, m6,
           phi_re, phi_im, hat_re, hat_im,
           g_re, g_im, w1, w2, w3, w4, w5, w6, rho, hat, phi, work,
           send1, send2, send3, send4, recv1, recv2, recv3, recv4,
           const_sem, in_sem, hat_sem, phi_sem, send_sem, recv_sem):
    py, pz = lax.axis_index("py"), lax.axis_index("pz")
    chunks = 2 * fields
    lane = lax.broadcasted_iota(jnp.int32, (32, 128), 1)

    def load(f, slot):
        return [pltpu.make_async_copy(src.at[f], rho.at[slot, c], in_sem.at[slot, c])
                for c, src in enumerate((rho_re, rho_im))]

    def store(dsts, buf, sem, i, slot):
        return [pltpu.make_async_copy(buf.at[slot, c], dst.at[i], sem.at[slot, c]) for c, dst in enumerate(dsts)]

    consts = [pltpu.make_async_copy(src, dst, const_sem.at[i]) for i, (src, dst) in enumerate(zip(
        (m1, m2, m3, m4, m5, m6, green_re, green_im), (w1, w2, w3, w4, w5, w6, g_re, g_im)))]
    for cp in load(0, 0) + consts:
        cp.start()

    barrier = pltpu.get_barrier_semaphore()
    for j in range(1, npy):
        pl.semaphore_signal(barrier, inc=1, device_id={"py": lax.rem(py + j, npy)}, device_id_type=MESH)
    for j in range(1, npz):
        pl.semaphore_signal(barrier, inc=1, device_id={"pz": lax.rem(pz + j, npz)}, device_id_type=MESH)
    pl.semaphore_wait(barrier, npy + npz - 2)
    for cp in consts:
        cp.wait()

    def exchange(stage, axis, send, recv, c):
        me, n = (py, npy) if axis == "py" else (pz, npz)
        rows = recv.shape[1] // n
        slot, ring = lax.rem(c, SLOTS), lax.rem(c, RING)
        mine = pl.ds(pl.multiple_of(me * rows, rows), rows)
        for j in range(1, n):
            to = lax.rem(me + j, n)
            pltpu.make_async_remote_copy(
                src_ref=send.at[slot, pl.ds(pl.multiple_of(to * rows, rows), rows), :], dst_ref=recv.at[ring, mine, :],
                send_sem=send_sem.at[stage, slot], recv_sem=recv_sem.at[stage, ring],
                device_id={axis: to}, device_id_type=MESH).start()
        pltpu.make_async_copy(send.at[slot, mine, :], recv.at[ring, mine, :], recv_sem.at[stage, ring]).start()

    def wait_sent(stage, axis, send, slot):
        n = npy if axis == "py" else npz
        part = send.at[slot, pl.ds(0, send.shape[1] // n * (n - 1)), :]
        pltpu.make_async_copy(part, part, send_sem.at[stage, slot]).wait()

    def wait_received(stage, recv, c):
        ring = lax.rem(c, RING)
        pltpu.make_async_copy(recv.at[ring], recv.at[ring], recv_sem.at[stage, ring]).wait()

    def step(u, carry):
        @pl.when((lax.rem(u, 2) == 0) & (u < chunks))
        def _():
            f = lax.div(u, 2)
            slot = lax.rem(f, 2)

            @pl.when(f + 1 < fields)
            def _():
                for cp in load(f + 1, 1 - slot):
                    cp.start()
            for cp in load(f, slot):
                cp.wait()
            volume = jnp.concatenate([rho[slot, 0], rho[slot, 1]], axis=1)
            for h in range(2):
                c = u + h
                to = lax.rem(c, SLOTS)

                @pl.when(c >= SLOTS)
                def _():
                    wait_sent(0, "py", send1, to)
                out = lax.dot_general(w1[h * 128:(h + 1) * 128, :], volume, (((1,), (1,)), ((), ())), precision=HIGHEST,
                                      preferred_element_type=jnp.float32)
                for p in range(8):
                    for t in range(4):
                        send1[to, p * 64 + t * 16:p * 64 + (t + 1) * 16, :] = out[p * 16:(p + 1) * 16, t * 128:(t + 1) * 128]
                exchange(0, "py", send1, recv1, c)

        @pl.when((u >= 2) & (u < chunks + 2))
        def _():
            c = u - 2
            to, ring = lax.rem(c, SLOTS), lax.rem(c, RING)
            wait_received(0, recv1, c)
            for part in range(2):
                for g in range(2):
                    blocks = [recv1[ring, pl.ds(part * 8 + 4 * g + k, 32, stride=16), :] for k in range(4)]
                    for y, b in enumerate(swap_blocks(blocks, lane)):
                        work[part * 128 + y * 32:part * 128 + (y + 1) * 32, g * 128:(g + 1) * 128] = b

            @pl.when(c >= SLOTS)
            def _():
                wait_sent(1, "pz", send2, to)
            send2[to] = jnp.dot(w2[...], work[...], precision=HIGHEST, preferred_element_type=jnp.float32)
            exchange(1, "pz", send2, recv2, c)

        @pl.when((u >= 4) & (u < chunks + 4))
        def _():
            c = u - 4
            to, ring, slot = lax.rem(c, SLOTS), lax.rem(c, RING), lax.rem(c, 2)
            wait_received(1, recv2, c)
            cols = []
            for part in range(2):
                rows = []
                for g in range(2):
                    blocks = [recv2[ring, b * 64 + part * 32:b * 64 + (part + 1) * 32, g * 128:(g + 1) * 128]
                              for b in range(4)]
                    rows += swap_blocks(blocks, lane)
                cols.append(jnp.concatenate(rows, axis=0))
            spec = jnp.dot(jnp.concatenate(cols, axis=1), w3[...], precision=HIGHEST, preferred_element_type=jnp.float32)
            sr, si = spec[:, :128], spec[:, 128:]

            @pl.when(c >= 2)
            def _():
                for cp in store((hat_re, hat_im), hat, hat_sem, c, slot):
                    cp.wait()

            @pl.when(c >= SLOTS)
            def _():
                wait_sent(2, "pz", send3, to)
            gr, gi = g_re[slot], g_im[slot]
            hat[slot, 0] = sr * gr - si * gi
            hat[slot, 1] = sr * gi + si * gr
            for cp in store((hat_re, hat_im), hat, hat_sem, c, slot):
                cp.start()
            back = jnp.dot(jnp.concatenate([hat[slot, 0], hat[slot, 1]], axis=1), w4[...], precision=HIGHEST,
                           preferred_element_type=jnp.float32)
            for part in range(2):
                for g in range(2):
                    blocks = [back[(4 * g + k) * 32:(4 * g + k + 1) * 32, part * 128:(part + 1) * 128] for k in range(4)]
                    for b, block in enumerate(swap_blocks(blocks, lane)):
                        send3[to, b * 64 + part * 32:b * 64 + (part + 1) * 32, g * 128:(g + 1) * 128] = block
            exchange(2, "pz", send3, recv3, c)

        @pl.when((u >= 6) & (u < chunks + 6))
        def _():
            c = u - 6
            to, ring = lax.rem(c, SLOTS), lax.rem(c, RING)
            wait_received(2, recv3, c)

            @pl.when(c >= SLOTS)
            def _():
                wait_sent(3, "py", send4, to)
            back = jnp.dot(w5[...], recv3[ring], precision=HIGHEST, preferred_element_type=jnp.float32)
            for part in range(2):
                for g in range(2):
                    blocks = [back[part * 128 + y * 32:part * 128 + (y + 1) * 32, g * 128:(g + 1) * 128] for y in range(4)]
                    for k, block in enumerate(swap_blocks(blocks, lane)):
                        send4[to, pl.ds(part * 8 + 4 * g + k, 32, stride=16), :] = block
            exchange(3, "py", send4, recv4, c)

        @pl.when((lax.rem(u, 2) == 0) & (u >= 8))
        def _():
            c = u - 8
            f = lax.div(c, 2)
            slot = lax.rem(f, 2)
            for h in range(2):
                wait_received(3, recv4, c + h)

            @pl.when(f >= 2)
            def _():
                for cp in store((phi_re, phi_im), phi, phi_sem, f, slot):
                    cp.wait()
            lines = []
            for t in range(4):
                block = jnp.concatenate([recv4[lax.rem(c + h, RING), p * 64 + t * 16:p * 64 + (t + 1) * 16, :]
                                         for h in range(2) for p in range(8)], axis=0)
                lines.append(block.T)
            out = jnp.dot(jnp.concatenate(lines, axis=0), w6[...], precision=HIGHEST, preferred_element_type=jnp.float32)
            phi[slot, 0] = out[:, :128]
            phi[slot, 1] = out[:, 128:]
            for cp in store((phi_re, phi_im), phi, phi_sem, f, slot):
                cp.start()

        return carry

    lax.fori_loop(0, chunks + 7, step, 0)
    for slot in range(2):
        for cp in store((hat_re, hat_im), hat, hat_sem, 0, slot) + store((phi_re, phi_im), phi, phi_sem, 0, slot):
            cp.wait()
    for slot in range(SLOTS):
        wait_sent(0, "py", send1, slot)
        wait_sent(1, "pz", send2, slot)
        wait_sent(2, "pz", send3, slot)
        wait_sent(3, "py", send4, slot)


def write_out(*refs):
    n = len(refs) // 2
    copies = [pltpu.make_async_copy(refs[i], refs[n + i], refs[-1].at[i]) for i in range(n)]
    for cp in copies:
        cp.start()
    for cp in copies:
        cp.wait()


def solution(mesh):
    npy, npz = mesh.shape["py"], mesh.shape["pz"]

    def local_solve(rho_re, rho_im, g_re, g_im):
        fields, n, ny, nz = rho_re.shape
        kx, ky = n // npy, n // npz
        fwd, inv = dft(n, -1), dft(n, 1)
        natural = np.arange(2 * n)
        x_blocks = order(n, (npy, 2, kx // 2), (2, 1, 0, 3))
        y_blocks = order(n, (npz, ky), (1, 0, 2))
        y_mixed = order(n, (npy, ny // 4, 4), (0, 3, 1, 2))
        pick = lambda m, r, c: jnp.asarray(m[np.ix_(r, c)].astype(np.float32))
        mats = (pick(fwd, x_blocks, natural), pick(fwd, y_blocks, y_mixed), pick(fwd.T, natural, natural),
                pick(inv.T, natural, natural), pick(inv, y_mixed, y_blocks), pick(inv.T, x_blocks, natural))
        lines = ny * nz
        half = lines // 2
        f32, any_space = jnp.float32, pl.BlockSpec(memory_space=pl.ANY)
        space = lambda v: v.transpose(0, 2, 3, 1).reshape(fields, lines, n)
        held = ((fields, lines, n),) * 2 + ((2 * fields, half, n),) * 2
        x_buf, y_buf = (lines, n), (2 * n, 2 * n)
        out = pl.pallas_call(
            functools.partial(kernel, fields, npy, npz),
            out_shape=[pltpu.VMEM(s, f32) for s in held],
            in_specs=[any_space] * 10,
            out_specs=[any_space] * 4,
            scratch_shapes=[pltpu.VMEM((2, half, n), f32)] * 2 + [pltpu.VMEM((2 * n, 2 * n), f32)] * 6 + [
                pltpu.VMEM((2, 2, lines, n), f32), pltpu.VMEM((2, 2, half, n), f32), pltpu.VMEM((2, 2, lines, n), f32),
                pltpu.VMEM(y_buf, f32)] + [
                pltpu.VMEM((SLOTS,) + b, f32) for b in (x_buf, y_buf, y_buf, x_buf)] + [
                pltpu.VMEM((RING,) + b, f32) for b in (x_buf, y_buf, y_buf, x_buf)] + [
                pltpu.SemaphoreType.DMA((8,)),
                pltpu.SemaphoreType.DMA((2, 2)), pltpu.SemaphoreType.DMA((2, 2)), pltpu.SemaphoreType.DMA((2, 2)),
                pltpu.SemaphoreType.DMA((4, SLOTS)), pltpu.SemaphoreType.DMA((4, RING)),
            ],
            compiler_params=pltpu.CompilerParams(collective_id=0, has_side_effects=True, vmem_limit_bytes=34 * 2**20),
        )(space(rho_re), space(rho_im), g_re.reshape(2, half, n), g_im.reshape(2, half, n), *mats)
        out = pl.pallas_call(
            write_out,
            out_shape=[jax.ShapeDtypeStruct(s, f32) for s in held],
            in_specs=[any_space] * 4, out_specs=[any_space] * 4,
            scratch_shapes=[pltpu.SemaphoreType.DMA((4,))],
            compiler_params=pltpu.CompilerParams(vmem_limit_bytes=2**20),
        )(*[pltpu.with_memory_space_constraint(v, pltpu.VMEM) for v in out])
        grid = lambda v: v.reshape(fields, ny, nz, n).transpose(0, 3, 1, 2)
        wave = lambda v: v.reshape(fields, kx, ky, n)
        return grid(out[0]), grid(out[1]), wave(out[2]), wave(out[3])

    space_layout = P("dp", None, "py", "pz")
    wave_layout = P("dp", "py", "pz", None)
    green_layout = P("py", "pz", None)
    return jax.shard_map(local_solve, mesh=mesh,
                         in_specs=(space_layout, space_layout, green_layout, green_layout),
                         out_specs=(space_layout, space_layout, wave_layout, wave_layout),
                         check_vma=False)
```

time: 325 us -> 305 us (0.938)
  local copies, waits for them, and re-layouts: 17.7 us -> 0 us
    unnamed x14 -> x0, local copies, waits for them, and re-layouts: 17.7 us -> none
    pallas_call x1 -> x2, Pallas kernels: 307 us -> 304 us  [the longest x1 296 us: local_solve(): pl.pallas_call(functools.partial(kernel, fields, npy, npz), out_shape=[pl...]
where the time goes in v2:
time: 305 us
  Pallas kernels  304 us (100%)
    pallas_call x1, Pallas kernels, local_solve(): pl.pallas_call(functools.partial(kernel, fields, npy, npz), out_shape=[pl...  296 us
    pallas_call x1, Pallas kernels, local_solve(): pl.pallas_call(write_out, out_shape=[jax.ShapeDtypeStruct(s, f32) for s i...  8.6 us

profile of v2, /device:TPU:97, one launch (start us, length us, event | category | flops | bytes accessed | tf_op | source)
XLA Modules:
  0.0 304.8 jit_solution(7426745436273841565)
XLA Ops:
  0.6 295.5 %shard_map.129 = (f32[24,512,128]{2,1,0:T(8,128)S(1)}, f32[24,512,128]{2,1,0:T(8,128)S(1)}, f32[48,256,128]{2,1,0:T(8,128)S(1)}, f32[48,256,128]{2,1,0:T(8,128)S(1)}) custom-call(f32[24,512,128]{2,1,0:T(8,128)} %bitcast.16, f32[24,512,128]{2,1,0:T(8,128)} %bitcast.17, f32[2,256,128]{2,1,0:T(8,128)} %bitcast.18, f32[2,256,128]{2,1,0:T(8,128)} %bitcast.19, ...), custom_call_target="tpu_custom_call" | custom-call | tf_op jit(solution)/shard_map/pallas_call | solution.py:254
  296.2 8.6 %shard_map.130 = (f32[24,512,128]{2,1,0:T(8,128)}, f32[24,512,128]{2,1,0:T(8,128)}, f32[48,256,128]{2,1,0:T(8,128)}, f32[48,256,128]{2,1,0:T(8,128)}) custom-call(f32[24,512,128]{2,1,0:T(8,128)S(1)} %get-tuple-element.12.refs_0_, f32[24,512,128]{2,1,0:T(8,128)S(1)} %get-tuple-element.13.refs_1_, f32[48,256,128]{2,1,0:T(8,128)S(1)} %get-tuple-element.14.refs_2_, ...), custom_call_target="tpu_custom_call" | custom-call | tf_op jit(solution)/shard_map/pallas_call | solution.py:270

commit v3 on v2

--- a/solution.py
+++ b/solution.py
@@ -35,11 +35,20 @@
     return a
 
 
+def last_dft(chunk, w):
+    lines = []
+    for t in range(4):
+        block = jnp.concatenate([chunk(h, slice(p * 64 + t * 16, p * 64 + (t + 1) * 16)) for h in range(2) for p in range(8)],
+                                axis=0)
+        lines.append(block.T)
+    return jnp.dot(jnp.concatenate(lines, axis=0), w[...], precision=HIGHEST, preferred_element_type=jnp.float32)
+
+
 def kernel(fields, npy, npz, rho_re, rho_im, green_re, green_im, m1, m2, m3, m4, m5, m6,
-           phi_re, phi_im, hat_re, hat_im,
-           g_re, g_im, w1, w2, w3, w4, w5, w6, rho, hat, phi, work,
-           send1, send2, send3, send4, recv1, recv2, recv3, recv4,
-           const_sem, in_sem, hat_sem, phi_sem, send_sem, recv_sem):
+           phi_re, phi_im, hat_re, hat_im, recv4,
+           g_re, g_im, w1, w2, w3, w4, w5, w6, rho, work,
+           send1, send2, send3, send4, recv1, recv2, recv3,
+           const_sem, in_sem, send_sem, recv_sem):
     py, pz = lax.axis_index("py"), lax.axis_index("pz")
     chunks = 2 * fields
     lane = lax.broadcasted_iota(jnp.int32, (32, 128), 1)
@@ -47,9 +56,6 @@
     def load(f, slot):
         return [pltpu.make_async_copy(src.at[f], rho.at[slot, c], in_sem.at[slot, c])
                 for c, src in enumerate((rho_re, rho_im))]
-
-    def store(dsts, buf, sem, i, slot):
-        return [pltpu.make_async_copy(buf.at[slot, c], dst.at[i], sem.at[slot, c]) for c, dst in enumerate(dsts)]
 
     consts = [pltpu.make_async_copy(src, dst, const_sem.at[i]) for i, (src, dst) in enumerate(zip(
         (m1, m2, m3, m4, m5, m6, green_re, green_im), (w1, w2, w3, w4, w5, w6, g_re, g_im)))]
@@ -61,16 +67,14 @@
         pl.semaphore_signal(barrier, inc=1, device_id={"py": lax.rem(py + j, npy)}, device_id_type=MESH)
     for j in range(1, npz):
         pl.semaphore_signal(barrier, inc=1, device_id={"pz": lax.rem(pz + j, npz)}, device_id_type=MESH)
-    pl.semaphore_wait(barrier, npy + npz - 2)
-    for cp in consts:
-        cp.wait()
+    consts[0].wait()
 
     def exchange(stage, axis, send, recv, c):
         me, n = (py, npy) if axis == "py" else (pz, npz)
         rows = recv.shape[1] // n
         slot, ring = lax.rem(c, SLOTS), lax.rem(c, RING)
         mine = pl.ds(pl.multiple_of(me * rows, rows), rows)
-        for j in range(1, n):
+        for j in sorted(range(1, n), key=lambda j: -min(j, n - j)):
             to = lax.rem(me + j, n)
             pltpu.make_async_remote_copy(
                 src_ref=send.at[slot, pl.ds(pl.multiple_of(to * rows, rows), rows), :], dst_ref=recv.at[ring, mine, :],
@@ -109,6 +113,12 @@
                     wait_sent(0, "py", send1, to)
                 out = lax.dot_general(w1[h * 128:(h + 1) * 128, :], volume, (((1,), (1,)), ((), ())), precision=HIGHEST,
                                       preferred_element_type=jnp.float32)
+                if h == 0:
+                    @pl.when(u == 0)
+                    def _():
+                        pl.semaphore_wait(barrier, npy + npz - 2)
+                        for cp in consts[1:]:
+                            cp.wait()
                 for p in range(8):
                     for t in range(4):
                         send1[to, p * 64 + t * 16:p * 64 + (t + 1) * 16, :] = out[p * 16:(p + 1) * 16, t * 128:(t + 1) * 128]
@@ -147,20 +157,13 @@
             spec = jnp.dot(jnp.concatenate(cols, axis=1), w3[...], precision=HIGHEST, preferred_element_type=jnp.float32)
             sr, si = spec[:, :128], spec[:, 128:]
 
-            @pl.when(c >= 2)
-            def _():
-                for cp in store((hat_re, hat_im), hat, hat_sem, c, slot):
-                    cp.wait()
-
             @pl.when(c >= SLOTS)
             def _():
                 wait_sent(2, "pz", send3, to)
             gr, gi = g_re[slot], g_im[slot]
-            hat[slot, 0] = sr * gr - si * gi
-            hat[slot, 1] = sr * gi + si * gr
-            for cp in store((hat_re, hat_im), hat, hat_sem, c, slot):
-                cp.start()
-            back = jnp.dot(jnp.concatenate([hat[slot, 0], hat[slot, 1]], axis=1), w4[...], precision=HIGHEST,
+            hat_re[c] = sr * gr - si * gi
+            hat_im[c] = sr * gi + si * gr
+            back = jnp.dot(jnp.concatenate([hat_re[c], hat_im[c]], axis=1), w4[...], precision=HIGHEST,
                            preferred_element_type=jnp.float32)
             for part in range(2):
                 for g in range(2):
@@ -190,31 +193,17 @@
         def _():
             c = u - 8
             f = lax.div(c, 2)
-            slot = lax.rem(f, 2)
             for h in range(2):
                 wait_received(3, recv4, c + h)
-
-            @pl.when(f >= 2)
-            def _():
-                for cp in store((phi_re, phi_im), phi, phi_sem, f, slot):
-                    cp.wait()
-            lines = []
-            for t in range(4):
-                block = jnp.concatenate([recv4[lax.rem(c + h, RING), p * 64 + t * 16:p * 64 + (t + 1) * 16, :]
-                                         for h in range(2) for p in range(8)], axis=0)
-                lines.append(block.T)
-            out = jnp.dot(jnp.concatenate(lines, axis=0), w6[...], precision=HIGHEST, preferred_element_type=jnp.float32)
-            phi[slot, 0] = out[:, :128]
-            phi[slot, 1] = out[:, 128:]
-            for cp in store((phi_re, phi_im), phi, phi_sem, f, slot):
-                cp.start()
+            out = last_dft(lambda h, rows: recv4[lax.rem(c + h, RING), rows, :], w6)
+            phi_re[f] = out[:, :128]
+            phi_im[f] = out[:, 128:]
 
         return carry
 
-    lax.fori_loop(0, chunks + 7, step, 0)
-    for slot in range(2):
-        for cp in store((hat_re, hat_im), hat, hat_sem, 0, slot) + store((phi_re, phi_im), phi, phi_sem, 0, slot):
-            cp.wait()
+    lax.fori_loop(0, chunks + 6, step, 0)
+    for c in range(chunks - 2, chunks):
+        wait_received(3, recv4, c)
     for slot in range(SLOTS):
         wait_sent(0, "py", send1, slot)
         wait_sent(1, "pz", send2, slot)
@@ -222,12 +211,23 @@
         wait_sent(3, "py", send4, slot)
 
 
-def write_out(*refs):
-    n = len(refs) // 2
-    copies = [pltpu.make_async_copy(refs[i], refs[n + i], refs[-1].at[i]) for i in range(n)]
-    for cp in copies:
+def write_out(phi_re, phi_im, hat_re, hat_im, recv4, m6, phi_re_out, phi_im_out, hat_re_out, hat_im_out, w6, last, sem):
+    fields = phi_re.shape[0]
+    weights = pltpu.make_async_copy(m6, w6, sem.at[6])
+    copies = [pltpu.make_async_copy(src, dst, sem.at[i]) for i, (src, dst) in enumerate((
+        (hat_re, hat_re_out), (hat_im, hat_im_out),
+        (phi_re.at[pl.ds(0, fields - 1)], phi_re_out.at[pl.ds(0, fields - 1)]),
+        (phi_im.at[pl.ds(0, fields - 1)], phi_im_out.at[pl.ds(0, fields - 1)])))]
+    for cp in [weights] + copies:
         cp.start()
-    for cp in copies:
+    weights.wait()
+    out = last_dft(lambda h, rows: recv4[(2 * (fields - 1) + h) % RING, rows, :], w6)
+    tail = [pltpu.make_async_copy(last.at[i], dst.at[fields - 1], sem.at[4 + i])
+            for i, dst in enumerate((phi_re_out, phi_im_out))]
+    for i, cp in enumerate(tail):
+        last[i] = out[:, i * 128:(i + 1) * 128]
+        cp.start()
+    for cp in copies + tail:
         cp.wait()
 
 
@@ -251,29 +251,29 @@
         space = lambda v: v.transpose(0, 2, 3, 1).reshape(fields, lines, n)
         held = ((fields, lines, n),) * 2 + ((2 * fields, half, n),) * 2
         x_buf, y_buf = (lines, n), (2 * n, 2 * n)
-        out = pl.pallas_call(
+        square, vmem = (2 * n, 2 * n), pl.BlockSpec(memory_space=pltpu.VMEM)
+        *out, tail = pl.pallas_call(
             functools.partial(kernel, fields, npy, npz),
-            out_shape=[pltpu.VMEM(s, f32) for s in held],
+            out_shape=[pltpu.VMEM(s, f32) for s in held + ((RING,) + x_buf,)],
             in_specs=[any_space] * 10,
-            out_specs=[any_space] * 4,
-            scratch_shapes=[pltpu.VMEM((2, half, n), f32)] * 2 + [pltpu.VMEM((2 * n, 2 * n), f32)] * 6 + [
-                pltpu.VMEM((2, 2, lines, n), f32), pltpu.VMEM((2, 2, half, n), f32), pltpu.VMEM((2, 2, lines, n), f32),
-                pltpu.VMEM(y_buf, f32)] + [
+            out_specs=[vmem] * 5,
+            scratch_shapes=[pltpu.VMEM((2, half, n), f32)] * 2 + [pltpu.VMEM(square, f32)] * 6 + [
+                pltpu.VMEM((2, 2, lines, n), f32), pltpu.VMEM(y_buf, f32)] + [
                 pltpu.VMEM((SLOTS,) + b, f32) for b in (x_buf, y_buf, y_buf, x_buf)] + [
-                pltpu.VMEM((RING,) + b, f32) for b in (x_buf, y_buf, y_buf, x_buf)] + [
-                pltpu.SemaphoreType.DMA((8,)),
-                pltpu.SemaphoreType.DMA((2, 2)), pltpu.SemaphoreType.DMA((2, 2)), pltpu.SemaphoreType.DMA((2, 2)),
+                pltpu.VMEM((RING,) + b, f32) for b in (x_buf, y_buf, y_buf)] + [
+                pltpu.SemaphoreType.DMA((8,)), pltpu.SemaphoreType.DMA((2, 2)),
                 pltpu.SemaphoreType.DMA((4, SLOTS)), pltpu.SemaphoreType.DMA((4, RING)),
             ],
-            compiler_params=pltpu.CompilerParams(collective_id=0, has_side_effects=True, vmem_limit_bytes=34 * 2**20),
-        )(space(rho_re), space(rho_im), g_re.reshape(2, half, n), g_im.reshape(2, half, n), *mats)
+            compiler_params=pltpu.CompilerParams(collective_id=0, has_side_effects=True, vmem_limit_bytes=22 * 2**20),
+        )(*[pltpu.with_memory_space_constraint(v, pltpu.HBM) for v in (
+            space(rho_re), space(rho_im), g_re.reshape(2, half, n), g_im.reshape(2, half, n), *mats)])
         out = pl.pallas_call(
             write_out,
             out_shape=[jax.ShapeDtypeStruct(s, f32) for s in held],
-            in_specs=[any_space] * 4, out_specs=[any_space] * 4,
-            scratch_shapes=[pltpu.SemaphoreType.DMA((4,))],
-            compiler_params=pltpu.CompilerParams(vmem_limit_bytes=2**20),
-        )(*[pltpu.with_memory_space_constraint(v, pltpu.VMEM) for v in out])
+            in_specs=[vmem] * 5 + [any_space], out_specs=[any_space] * 4,
+            scratch_shapes=[pltpu.VMEM(square, f32), pltpu.VMEM((2, lines, n), f32), pltpu.SemaphoreType.DMA((7,))],
+            compiler_params=pltpu.CompilerParams(vmem_limit_bytes=4 * 2**20),
+        )(*[pltpu.with_memory_space_constraint(v, pltpu.VMEM) for v in (*out, tail)], mats[5])
         grid = lambda v: v.reshape(fields, ny, nz, n).transpose(0, 3, 1, 2)
         wave = lambda v: v.reshape(fields, kx, ky, n)
         return grid(out[0]), grid(out[1]), wave(out[2]), wave(out[3])

time: 305 us -> 303 us (level)
  no operation moved by 1% of the time
where the time goes in v3:
time: 303 us
  Pallas kernels  302 us (100%)
    pallas_call x1, Pallas kernels, local_solve(): pl.pallas_call(functools.partial(kernel, fields, npy, npz), out_shape=[pl...  293 us
    pallas_call x1, Pallas kernels, local_solve(): pl.pallas_call(write_out, out_shape=[jax.ShapeDtypeStruct(s, f32) for s i...  8.48 us

profile of v3, /device:TPU:97, one launch (start us, length us, event | category | flops | bytes accessed | tf_op | source)
XLA Modules:
  0.0 302.6 jit_solution(1623141101210480064)
XLA Ops:
  0.6 0.0 copy-start
  0.6 293.4 %shard_map.129 = (f32[24,512,128]{2,1,0:T(8,128)S(1)}, f32[24,512,128]{2,1,0:T(8,128)S(1)}, f32[48,256,128]{2,1,0:T(8,128)S(1)}, f32[48,256,128]{2,1,0:T(8,128)S(1)}, f32[8,512,128]{2,1,0:T(8,128)S(1)}) custom-call(f32[24,512,128]{2,1,0:T(8,128)} %bitcast.16, f32[24,512,128]{2,1,0:T(8,128)} %bitcast.17, f32[2,256,128]{2,1,0:T(8,128)} %bitcast.18, ...), custom_call_target="tpu_custom_call" | custom-call | tf_op jit(solution)/shard_map/pallas_call | solution.py:255
  294.1 0.0 copy-done
  294.1 8.5 %shard_map.130 = (f32[24,512,128]{2,1,0:T(8,128)}, f32[24,512,128]{2,1,0:T(8,128)}, f32[48,256,128]{2,1,0:T(8,128)}, f32[48,256,128]{2,1,0:T(8,128)}) custom-call(f32[24,512,128]{2,1,0:T(8,128)S(1)} %get-tuple-element.13.phi_re, f32[24,512,128]{2,1,0:T(8,128)S(1)} %get-tuple-element.14.phi_im, f32[48,256,128]{2,1,0:T(8,128)S(1)} %get-tuple-element.15.hat_re, ...), custom_call_target="tpu_custom_call" | custom-call | tf_op jit(solution)/shard_map/pallas_call | solution.py:270
Async XLA Ops:
  0.6 293.4 %copy-start = (f32[256,256]{1,0:T(8,128)S(1)}, f32[256,256]{1,0:T(8,128)}, u32[]{:S(2)}) copy-start(f32[256,256]{1,0:T(8,128)} %constant.10.clone.m1.m6) | copy-start | bytes 786436
